TPU v7x, 32 devices: a whole 2x2x4 slice. The times are simulated.
32 devices in a mesh: gx: 4 (over y, x), gy: 8 (over z, core).
Axes of the slice: x: 2, y: 2, z: 4, core: 2. Of those that a mesh axis runs over, the one named last changes fastest.
Arguments:
- volume: float32 [128, 512, 256], P('gx', 'gy'), may hold values from -18 to 18, as said below
Outputs:
- denoised: float32 [128, 512, 256], P('gx', 'gy')
Inputs may be any that keep to these rules, and one draw needn't show every extreme that they name: `volume`: real values.
All inputs are finite; a program needn't handle non-finite values.
Results may differ from a plain program's by a relative error of at most 0.00002.
Values sent between devices are 32-bit elements; how exact they have to be, the bound alone decides.
A program may use at most 128 MiB of HBM per device.

v0:
```python
import functools
import math

import jax
import jax.numpy as jnp
import numpy as np
from jax import lax
from jax.experimental import pallas as pl
from jax.experimental.pallas import tpu as pltpu
from jax.sharding import PartitionSpec as P

ROOT3 = math.sqrt(3.0)
NEAR = math.sqrt(3.0) / 4.0
FAR = (math.sqrt(3.0) - 2.0) / 4.0
LOW = (math.sqrt(3.0) - 1.0) / math.sqrt(2.0)
HIGH = (math.sqrt(3.0) + 1.0) / math.sqrt(2.0)
LANES = 128
PAD = 8


def forward_matrix(size):
    lines = np.eye(size)
    even, odd = lines[:, 0::2], lines[:, 1::2]
    smooth = even + ROOT3 * odd
    detail = odd - NEAR * smooth - FAR * np.roll(smooth, 1, 1)
    smooth = smooth - np.roll(detail, -1, 1)
    return np.concatenate([LOW * smooth, HIGH * detail], 1)


def inverse_matrix(size):
    lines = np.eye(size)
    smooth, detail = lines[:, : size // 2] / LOW, lines[:, size // 2 :] / HIGH
    first = smooth + np.roll(detail, -1, 1)
    odd = detail + NEAR * first + FAR * np.roll(first, 1, 1)
    even = first - ROOT3 * odd
    return np.stack([even, odd], 2).reshape(size, size)


def halves(matrix, size):
    full = np.zeros((size, size))
    full[: matrix.shape[0], : matrix.shape[1]] = matrix
    high = full.astype(jnp.bfloat16)
    low = (full - high.astype(np.float64)).astype(jnp.bfloat16)
    return np.stack([high, low])


def times(values, w_ref):
    high = values.astype(jnp.bfloat16)
    low = (values - high.astype(jnp.float32)).astype(jnp.bfloat16)
    dot = functools.partial(jnp.dot, preferred_element_type=jnp.float32)
    return dot(high, w_ref[0]) + (dot(low, w_ref[0]) + dot(high, w_ref[1]))


def shrink(values, noise):
    return values - jnp.clip(values, -noise, noise)


def sums(even, odd):
    smooth = even + ROOT3 * odd
    return smooth, odd - NEAR * smooth


def undo(detail, first, before):
    odd = detail + NEAR * first + FAR * before
    return first - ROOT3 * odd, odd


def weave(even, odd):
    both = jnp.stack([even, odd], axis=1)
    return both.reshape((2 * even.shape[0],) + even.shape[1:])


def forward_x(src, halo, det, smo, count):
    smooth, part = sums(src[0], src[1])
    det[0] = HIGH * (part - FAR * halo[0])

    def step(n, carry):
        before, _ = sums(src[2 * n - 2], src[2 * n - 1])
        smooth, part = sums(src[2 * n], src[2 * n + 1])
        detail = part - FAR * before
        det[n] = HIGH * detail
        smo[n - 1] = LOW * (before - detail)
        return carry

    lax.fori_loop(1, count, step, 0)
    last, _ = sums(src[2 * count - 2], src[2 * count - 1])
    smo[count - 1] = LOW * (last - (halo[1] - FAR * last))


def forward_y(load, count):
    s0, t0 = sums(load(PAD), load(PAD + 1))
    sm, _ = sums(load(PAD - 2), load(PAD - 1))
    sp, tp = sums(load(PAD + 2), load(PAD + 3))
    return HIGH * (t0 - FAR * sm), LOW * (s0 - (tp - FAR * s0))


def kernel(shape, count_all, nx, ny, vol, w1, w2, w3, v1, v2, v3, out,
           e1, hx1, sx1, xd1, xs1, s1s, s1d, d1s, d1d,
           e2, hx2, sx2, xd2, xs2, ss, sd, ds, dd, t3d, t3s, r2, r1,
           p1s, p1d, o1, ob, part, total, line, send, recv, lsem, osem):
    cx, cy, cz = shape
    ix, iy = lax.axis_index("gx"), lax.axis_index("gy")

    def device(dx, dy):
        return (lax.rem(ix + dx + nx, nx), lax.rem(iy + dy + ny, ny))

    loads = [
        pltpu.make_async_copy(
            vol.at[:, :, pl.ds(h * LANES, LANES)],
            e1.at[:, h, pl.ds(PAD, cy), :], lsem.at[h])
        for h in range(2)
    ]
    for c in loads:
        c.start()

    greet = [(dx, dy) for dx in (-1, 0, 1) for dy in (-1, 0, 1) if dx or dy]
    greet += [(dx, 0) for dx in range(2, nx - 1)] + [(0, dy) for dy in range(2, ny - 1)]
    barrier = pltpu.get_barrier_semaphore()
    for d in greet:
        pl.semaphore_signal(barrier, inc=1, device_id=device(*d),
                            device_id_type=pl.DeviceIdType.MESH)
    pl.semaphore_wait(barrier, len(greet))

    slot = [0]
    started = []

    def post(src, dst, dx, dy):
        n = slot[0]
        slot[0] += 1
        c = pltpu.make_async_remote_copy(
            src_ref=src, dst_ref=dst, send_sem=send.at[n], recv_sem=recv.at[n],
            device_id=device(dx, dy), device_id_type=pl.DeviceIdType.MESH)
        c.start()
        started.append(c)
        return c

    for c in loads:
        c.wait()

    low, high = pl.ds(0, PAD), pl.ds(PAD + cy, PAD)
    first, last = pl.ds(PAD, PAD), pl.ds(cy, PAD)
    sx1[0] = sums(e1[cx - 2, :, PAD : PAD + cy], e1[cx - 1, :, PAD : PAD + cy])[0]
    sx1[1] = sums(e1[0, :, PAD : PAD + cy], e1[1, :, PAD : PAD + cy])[1]
    round1 = []
    for side, dx in ((0, 1), (1, -1)):
        round1 += [
            post(sx1.at[side], hx1.at[side, :, pl.ds(PAD, cy), :], dx, 0),
            post(sx1.at[side, :, pl.ds(cy - PAD, PAD), :], hx1.at[side, :, low, :], dx, 1),
            post(sx1.at[side, :, pl.ds(0, PAD), :], hx1.at[side, :, high, :], dx, -1),
        ]
    round1 += [
        post(e1.at[:, :, last, :], e1.at[:, :, low, :], 0, 1),
        post(e1.at[:, :, first, :], e1.at[:, :, high, :], 0, -1),
    ]
    for c in round1:
        c.wait_recv()
    hx, hy = cx // 2, cy // 2
    forward_x(e1, hx1, xd1, xs1, hx)

    def cols1(n, carry):
        for h in range(2):
            for src, det, smo, at in ((xd1, d1d, d1s, n), (xs1, s1d, s1s, n + 1)):
                d, s = forward_y(
                    lambda start: src[n, h, pl.ds(start, hy, stride=2), :], hy)
                det[at, h, 0:hy] = d
                smo[at, h, PAD : PAD + hy] = s
        return carry

    lax.fori_loop(0, hx, cols1, 0)

    chunk = hx // 2

    def depth1(ref, x0, y0, extra=None):
        rows = jnp.concatenate(
            [ref[pl.ds(x0, chunk), h, y0 : y0 + hy].reshape(chunk * hy, LANES) for h in range(2)],
            axis=1)
        got = times(rows, w1)
        parts = [got[:, h * LANES : (h + 1) * LANES].reshape(chunk, hy, LANES) for h in range(2)]
        for h in range(2):
            ref[pl.ds(x0, chunk), h, y0 : y0 + hy] = parts[h]
        return parts

    magnitude = jnp.zeros((PAD, LANES), jnp.float32)
    for i in range(2):
        parts = depth1(s1s, 1 + i * chunk, PAD)
        e2[i * chunk : (i + 1) * chunk, PAD : PAD + hy] = parts[0]

    low2, high2 = pl.ds(0, PAD), pl.ds(PAD + hy, PAD)
    sx2[0] = sums(e2[hx - 2, PAD : PAD + hy], e2[hx - 1, PAD : PAD + hy])[0]
    sx2[1] = sums(e2[0, PAD : PAD + hy], e2[1, PAD : PAD + hy])[1]
    round2 = []
    for side, dx in ((0, 1), (1, -1)):
        round2 += [
            post(sx2.at[side], hx2.at[side, pl.ds(PAD, hy), :], dx, 0),
            post(sx2.at[side, pl.ds(hy - PAD, PAD), :], hx2.at[side, low2, :], dx, 1),
            post(sx2.at[side, pl.ds(0, PAD), :], hx2.at[side, high2, :], dx, -1),
        ]
    round2 += [
        post(e2.at[:, pl.ds(hy, PAD), :], e2.at[:, low2, :], 0, 1),
        post(e2.at[:, pl.ds(PAD, PAD), :], e2.at[:, high2, :], 0, -1),
    ]

    for i in range(2):
        depth1(s1d, 1 + i * chunk, 0)
        depth1(d1s, i * chunk, PAD)
        parts = depth1(d1d, i * chunk, 0)
        magnitude = magnitude + jnp.sum(
            jnp.abs(parts[1]).reshape(chunk * hy // PAD, PAD, LANES), axis=0)

    part[0] = magnitude
    sums_x = [post(part.at[0], part.at[k], k, 0) for k in range(1, nx)]

    for c in round2:
        c.wait_recv()
    qx, qy = hx // 2, hy // 2
    forward_x(e2, hx2, xd2, xs2, qx)

    def cols2(n, carry):
        for src, det, smo, at_d, at_s in (
            (xd2, dd, ds, n + 1, n + 1), (xs2, sd, ss, n + 2, n + 4)):
            d, s = forward_y(lambda start: src[n, pl.ds(start, qy, stride=2), :], qy)
            det[at_d, PAD : PAD + qy] = d
            smo[at_s, PAD : PAD + qy] = s
        return carry

    lax.fori_loop(0, qx, cols2, 0)

    def depth2(ref, x0):
        rows = ref[x0 : x0 + qx, PAD : PAD + qy].reshape(qx * qy, LANES)
        ref[x0 : x0 + qx, PAD : PAD + qy] = times(rows, w2).reshape(qx, qy, LANES)

    depth2(ss, 4)
    depth2(sd, 2)
    depth2(ds, 1)
    depth2(dd, 1)

    def spread(ref, own, lows, highs, up, down):
        posts = []
        rows = {0: (pl.ds(PAD, qy), pl.ds(PAD, qy))}
        if up:
            rows[1] = (pl.ds(qy, PAD), pl.ds(0, PAD))
        if down:
            rows[-1] = (pl.ds(PAD, PAD), pl.ds(PAD + qy, PAD))
        layers = {0: (pl.ds(own, qx), pl.ds(own, qx))}
        if lows:
            layers[1] = (pl.ds(own + qx - lows, lows), pl.ds(own - lows, lows))
        if highs:
            layers[-1] = (pl.ds(own, highs), pl.ds(own + qx, highs))
        for dx, (xsrc, xdst) in layers.items():
            for dy, (ysrc, ydst) in rows.items():
                if dx or dy:
                    posts.append(post(ref.at[xsrc, ysrc, :], ref.at[xdst, ydst, :], dx, dy))
        return posts

    round3 = spread(ss, 4, 4, 2, True, True)
    for c in sums_x:
        c.wait_recv()
    acc = part[0]
    for k in range(1, nx):
        acc = acc + part[k]
    total[0] = acc
    sums_y = [post(total.at[0], total.at[k], 0, k) for k in range(1, ny)]
    round4 = spread(sd, 2, 2, 0, True, True)
    round4 += spread(ds, 1, 1, 1, True, False)
    round4 += spread(dd, 1, 1, 1, True, True)

    ends = []
    for ref, own, dx in ((s1s, 1, 1), (s1d, 1, 1), (d1s, 0, -1), (d1d, 0, -1)):
        smooth = ref is s1s or ref is d1s
        x_all = pl.ds(own, hx)
        y_all = pl.ds(PAD if smooth else 0, hy)
        x_src, x_dst = (hx, 0) if dx == 1 else (0, hx)
        y_src, y_dst = (pl.ds(hy, PAD), pl.ds(0, PAD)) if smooth else (pl.ds(0, PAD), pl.ds(hy, PAD))
        dy = 1 if smooth else -1
        lanes = pl.ds(1, 1) if ref is s1s else pl.ds(0, 2)
        ends += [
            post(ref.at[pl.ds(x_src, 1), lanes, y_all, :], ref.at[pl.ds(x_dst, 1), lanes, y_all, :], dx, 0),
            post(ref.at[x_all, lanes, y_src, :], ref.at[x_all, lanes, y_dst, :], 0, dy),
            post(ref.at[pl.ds(x_src, 1), lanes, y_src, :], ref.at[pl.ds(x_dst, 1), lanes, y_dst, :], dx, dy),
        ]

    for c in round3:
        c.wait_recv()
    low_s, low_t = [], []
    for n in range(qx // 2 + 3):
        s, t = sums(ss[2 * n], ss[2 * n + 1])
        low_s.append(s)
        low_t.append(t)
    n3 = qx // 2 + 2
    for n in range(n3):
        detail = low_t[n + 1] - FAR * low_s[n]
        t3d[n] = HIGH * detail
        t3s[n] = LOW * (low_s[n] - detail)
    h3 = qy // 2 + PAD
    bands = []
    for src in (t3d, t3s):
        s, t = sums(src[:, pl.ds(0, h3, stride=2), :], src[:, pl.ds(1, h3, stride=2), :])
        d = t - FAR * pltpu.roll(s, 1, 1)
        s = s - pltpu.roll(d, h3 - 1, 1)
        bands += [HIGH * d, LOW * s]
    for i, band in enumerate(bands):
        bands[i] = times(band.reshape(n3 * h3, LANES), w3).reshape(n3, h3, LANES)

    for c in sums_y:
        c.wait_recv()
    acc = total[0]
    for k in range(1, ny):
        acc = acc + total[k]
    noise = jnp.sum(acc, axis=(0, 1), keepdims=True) * (math.sqrt(math.pi / 2.0) / count_all)
    line[...] = jnp.broadcast_to(noise, (PAD, LANES))

    lane3 = lax.broadcasted_iota(jnp.int32, (n3, h3, LANES), 2)
    noise3 = noise.reshape(1, 1, 1)
    b_dd, b_ds, b_sd = (shrink(b, noise3) for b in bands[:3])
    b_ss = jnp.where(lane3 < cz // 8, bands[3], shrink(bands[3], noise3))

    def inverse_x(det, smo):
        det, smo = det * (1.0 / HIGH), smo * (1.0 / LOW)
        one = smo + det
        even, odd = undo(det[:-1], one[1:], one[:-1])
        return weave(even, odd)

    y_d = inverse_x(b_dd, b_sd) * (1.0 / HIGH)
    y_s = inverse_x(b_ds, b_ss) * (1.0 / LOW)
    one = y_s + pltpu.roll(y_d, h3 - 1, 1)
    even, odd = undo(y_d, one, pltpu.roll(one, 1, 1))
    r2[:, pl.ds(0, h3, stride=2), :] = even
    r2[:, pl.ds(1, h3, stride=2), :] = odd
    x2, yrows = qx + 2, qy + 2 * PAD
    back = times(r2[...].reshape(x2 * yrows, LANES), v3).reshape(x2, yrows, LANES)

    for c in round4:
        c.wait_recv()
    for c in round3:
        c.wait_send()
    lane2 = lax.broadcasted_iota(jnp.int32, (x2, yrows, LANES), 2)
    ss[2 : 2 + x2] = jnp.where(lane2 < cz // 4, back, shrink(ss[2 : 2 + x2], noise3))
    noise2 = noise

    def inv2(n, carry):
        def one_x(n):
            d_d = shrink(dd[n], noise2) * (1.0 / HIGH)
            d_s = shrink(ds[n], noise2) * (1.0 / HIGH)
            s_d = shrink(sd[n], noise2) * (1.0 / LOW)
            s_s = ss[n + 2] * (1.0 / LOW)
            return d_d, d_s, s_d + d_d, s_s + d_s

        d_d, d_s, b_d, b_s = one_x(n)
        _, _, f_d, f_s = one_x(n + 1)
        pair_d = undo(d_d, f_d, b_d)
        pair_s = undo(d_s, f_s, b_s)
        for i in range(2):
            y_d, y_s = pair_d[i] * (1.0 / HIGH), pair_s[i] * (1.0 / LOW)
            one = y_s + pltpu.roll(y_d, yrows - 1, 0)
            even, odd = undo(y_d, one, pltpu.roll(one, 1, 0))
            r1[2 * n + i, pl.ds(0, yrows, stride=2), :] = even
            r1[2 * n + i, pl.ds(1, yrows, stride=2), :] = odd
        return carry

    lax.fori_loop(0, qx + 1, inv2, 0)
    x1, y1 = hx + 2, hy + PAD
    back = times(r1[:, PAD : PAD + y1].reshape(x1 * y1, LANES), v2).reshape(x1, y1, LANES)
    s1s[:, 0] = back[1:]

    for c in ends:
        c.wait_recv()

    def inv1(n, carry):
        for h in range(2):
            for det, smo, dst in ((d1d, s1d, p1d), (d1s, s1s, p1s)):
                plain = smo is s1s and h == 0

                def one_x(n):
                    d = shrink(det[n, h], noise2) * (1.0 / HIGH)
                    s = smo[n, h] if plain else shrink(smo[n, h], noise2)
                    return d, s * (1.0 / LOW) + d

                d, before = one_x(n)
                _, one = one_x(n + 1)
                even, odd = undo(d, one, before)
                dst[2 * n, h] = even
                dst[2 * n + 1, h] = odd
        return carry

    lax.fori_loop(0, hx, inv1, 0)

    def inv1_y(n, carry):
        for h in range(2):
            y_d = p1d[n, h, 0:hy] * (1.0 / HIGH)
            y_n = p1d[n, h, 1 : hy + 1] * (1.0 / HIGH)
            s = p1s[n, h, PAD : PAD + hy] * (1.0 / LOW)
            s_b = p1s[n, h, PAD - 1 : PAD - 1 + hy] * (1.0 / LOW)
            even, odd = undo(y_d, s + y_n, s_b + y_d)
            o1[n, h, pl.ds(0, hy, stride=2), :] = even
            o1[n, h, pl.ds(1, hy, stride=2), :] = odd
        return carry

    lax.fori_loop(0, cx, inv1_y, 0)
    layers = 8
    outs = []
    for i in range(cx // layers):
        xs = slice(i * layers, (i + 1) * layers)
        rows = jnp.concatenate(
            [o1[xs, h].reshape(layers * cy, LANES) for h in range(2)], axis=1)
        ob[xs] = times(rows, v1).reshape(layers, cy, cz)
        c = pltpu.make_async_copy(ob.at[xs], out.at[xs], osem.at[i])
        c.start()
        outs.append(c)
    for c in outs:
        c.wait()
    early = [id(c) for c in round3]
    for c in started:
        if id(c) not in early:
            c.wait_send()


def on_device(nx, ny, volume):
    cx, cy, cz = volume.shape
    hx, hy, qx, qy = cx // 2, cy // 2, cx // 4, cy // 4
    n3, h3 = qx // 2 + 2, qy // 2 + PAD
    f32 = jnp.float32
    count = cx * nx * cy * ny * cz // 8
    weights = [
        halves(forward_matrix(cz), cz), halves(forward_matrix(cz // 2), LANES),
        halves(forward_matrix(cz // 4), LANES), halves(inverse_matrix(cz), cz),
        halves(inverse_matrix(cz // 2), LANES), halves(inverse_matrix(cz // 4), LANES),
    ]
    messages = 8 + 8 + 26 + 12 + nx - 1 + ny - 1
    vmem = lambda *s: pltpu.VMEM(s, f32)
    scratch = [
        vmem(cx, 2, cy + 2 * PAD, LANES), vmem(2, 2, cy + 2 * PAD, LANES), vmem(2, 2, cy, LANES),
        vmem(hx, 2, cy + 2 * PAD, LANES), vmem(hx, 2, cy + 2 * PAD, LANES),
        *[vmem(hx + 1, 2, hy + PAD, LANES) for _ in range(4)],
        vmem(hx, hy + 2 * PAD, LANES), vmem(2, hy + 2 * PAD, LANES), vmem(2, hy, LANES),
        vmem(qx, hy + 2 * PAD, LANES), vmem(qx, hy + 2 * PAD, LANES),
        vmem(qx + 6, qy + 2 * PAD, LANES),
        *[vmem(qx + 2, qy + 2 * PAD, LANES) for _ in range(3)],
        vmem(n3, qy + 2 * PAD, LANES), vmem(n3, qy + 2 * PAD, LANES),
        vmem(qx + 2, qy + 2 * PAD, LANES),
        vmem(hx + 2, 2 * (qy + 2 * PAD), LANES),
        vmem(cx, 2, hy + PAD, LANES), vmem(cx, 2, hy + PAD, LANES),
        vmem(cx, 2, cy, LANES), vmem(cx, cy, cz),
        vmem(nx, PAD, LANES), vmem(ny, PAD, LANES), vmem(PAD, LANES),
        pltpu.SemaphoreType.DMA((messages,)), pltpu.SemaphoreType.DMA((messages,)),
        pltpu.SemaphoreType.DMA((2,)), pltpu.SemaphoreType.DMA((cx // 8,)),
    ]
    return pl.pallas_call(
        functools.partial(kernel, (cx, cy, cz), count, nx, ny),
        out_shape=jax.ShapeDtypeStruct(volume.shape, f32),
        in_specs=[pl.BlockSpec(memory_space=pl.ANY)]
        + [pl.BlockSpec(memory_space=pltpu.VMEM)] * 6,
        out_specs=pl.BlockSpec(memory_space=pl.ANY),
        scratch_shapes=scratch,
        compiler_params=pltpu.CompilerParams(
            collective_id=0, has_side_effects=True, vmem_limit_bytes=56 * 1024 * 1024),
    )(volume, *[jnp.asarray(w) for w in weights])


def solution(mesh):
    spec = P("gx", "gy", None)
    body = functools.partial(on_device, mesh.shape["gx"], mesh.shape["gy"])
    return jax.shard_map(body, mesh=mesh, in_specs=(spec,), out_specs=spec, check_vma=False)
```

profile of v0, /device:TPU:0, one launch (start us, length us, event | category | flops | bytes accessed | tf_op | source)
XLA Modules:
  0.0 41.5 jit_solution(9738744062203226273)
XLA Ops:
  0.0 38.4 %shard_map.73 = f32[32,64,256]{2,1,0:T(8,128)} custom-call(f32[32,64,256]{2,1,0:T(8,128)} %vol.1, bf16[2,256,256]{2,1,0:T(8,128)(2,1)} %constant.12.clone.w1, bf16[2,128,128]{2,1,0:T(8,128)(2,1)} %constant.13.clone.w2, bf16[2,128,128]{2,1,0:T(8,128)(2,1)} %constant.14.clone.w3, bf16[2,256,256]{2,1,0:T(8,128)(2,1)} %constant.15.clone.v1, ...), custom_call_target="tpu_custom_call" | custom-call | tf_op jit(solution)/shard_map/pallas_call | solution.py:447
  38.4 3.1 %copy.9 = f32[32,64,256]{2,1,0:T(8,128)} copy(f32[32,64,256]{2,1,0:T(8,128)} %shard_map.73) | data formatting | bytes 4194304
where the time goes:
time: 41.7 us; the launch traced here: 41.5 us
  Pallas kernels  38.4 us (92%)
  local copies, waits for them, and re-layouts  3.13 us (8%)
    pallas_call x1, Pallas kernels, on_device(): pl.pallas_call(functools.partial(kernel, (cx, cy, cz), count, nx, ny), ou...  38.4 us
    unnamed x1, local copies, waits for them, and re-layouts  3.13 us

commit v1 on v0

v1 whole, which is shorter than its diff:
```python
import functools
import math

import jax
import jax.numpy as jnp
import numpy as np
from jax import lax
from jax.experimental import pallas as pl
from jax.experimental.pallas import tpu as pltpu
from jax.sharding import PartitionSpec as P

ROOT3 = math.sqrt(3.0)
NEAR = math.sqrt(3.0) / 4.0
FAR = (math.sqrt(3.0) - 2.0) / 4.0
LOW = (math.sqrt(3.0) - 1.0) / math.sqrt(2.0)
HIGH = (math.sqrt(3.0) + 1.0) / math.sqrt(2.0)
LANES = 128
PAD = 8


def forward_matrix(size):
    lines = np.eye(size)
    even, odd = lines[:, 0::2], lines[:, 1::2]
    smooth = even + ROOT3 * odd
    detail = odd - NEAR * smooth - FAR * np.roll(smooth, 1, 1)
    smooth = smooth - np.roll(detail, -1, 1)
    return np.concatenate([LOW * smooth, HIGH * detail], 1)


def inverse_matrix(size):
    lines = np.eye(size)
    smooth, detail = lines[:, : size // 2] / LOW, lines[:, size // 2 :] / HIGH
    first = smooth + np.roll(detail, -1, 1)
    odd = detail + NEAR * first + FAR * np.roll(first, 1, 1)
    even = first - ROOT3 * odd
    return np.stack([even, odd], 2).reshape(size, size)


def halves(matrix, size):
    full = np.zeros((size, size))
    full[: matrix.shape[0], : matrix.shape[1]] = matrix
    high = full.astype(jnp.bfloat16)
    low = (full - high.astype(np.float64)).astype(jnp.bfloat16)
    return np.stack([high, low])


def times(values, w_ref):
    high = values.astype(jnp.bfloat16)
    low = (values - high.astype(jnp.float32)).astype(jnp.bfloat16)
    dot = functools.partial(jnp.dot, preferred_element_type=jnp.float32)
    return dot(high, w_ref[0]) + (dot(low, w_ref[0]) + dot(high, w_ref[1]))


def shrink(values, noise):
    return values - jnp.clip(values, -noise, noise)


def sums(even, odd):
    smooth = even + ROOT3 * odd
    return smooth, odd - NEAR * smooth


def undo(detail, first, before):
    odd = detail + NEAR * first + FAR * before
    return first - ROOT3 * odd, odd


def weave(even, odd):
    both = jnp.stack([even, odd], axis=1)
    return both.reshape((2 * even.shape[0],) + even.shape[1:])


def forward_rows(even, odd):
    axis = even.ndim - 2
    smooth, part = sums(even, odd)
    detail = part - FAR * pltpu.roll(smooth, 1, axis)
    return HIGH * detail, LOW * (smooth - pltpu.roll(detail, even.shape[axis] - 1, axis))


def kernel(shape, count_all, nx, ny, vol, w1, w2, w3, v1, v2, v3, out,
           e1, hx1, sx1, hy1, sy1, hc1, sc1, xd1, xs1, s1s, s1d, d1s, d1d,
           e2, ht2, st2, xd2, xs2, ss, sd, ds, dd, ep3, t3d, t3s, r2, r1,
           p1s, p1d, o1, ob, part, total, send, recv, lsem, osem):
    cx, cy, cz = shape
    hx, hy, qx, qy = cx // 2, cy // 2, cx // 4, cy // 4
    ix, iy = lax.axis_index("gx"), lax.axis_index("gy")

    def device(dx, dy):
        return (lax.rem(ix + dx + nx, nx), lax.rem(iy + dy + ny, ny))

    loads = [
        pltpu.make_async_copy(
            vol.at[:, :, pl.ds(h * LANES, LANES)],
            e1.at[:, h, pl.ds(PAD, cy), :], lsem.at[h])
        for h in range(2)
    ]
    for c in loads:
        c.start()

    greet = [(dx, dy) for dx in (-1, 0, 1) for dy in (-1, 0, 1) if dx or dy]
    greet += [(dx, 0) for dx in range(2, nx - 1)] + [(0, dy) for dy in range(2, ny - 1)]
    barrier = pltpu.get_barrier_semaphore()
    for d in greet:
        pl.semaphore_signal(barrier, inc=1, device_id=device(*d),
                            device_id_type=pl.DeviceIdType.MESH)

    slot = [0]
    started = []

    def post(src, dst, dx, dy):
        n = slot[0]
        slot[0] += 1
        c = pltpu.make_async_remote_copy(
            src_ref=src, dst_ref=dst, send_sem=send.at[n], recv_sem=recv.at[n],
            device_id=device(dx, dy), device_id_type=pl.DeviceIdType.MESH)
        c.start()
        started.append(c)
        return c

    for c in loads:
        c.wait()

    top = PAD + cy
    sx1[1] = sums(e1[0, :, PAD:top], e1[1, :, PAD:top])[1]
    sy1[1] = sums(e1[:, :, PAD : PAD + 1], e1[:, :, PAD + 1 : PAD + 2])[1]
    sx1[0] = sums(e1[cx - 2, :, PAD:top], e1[cx - 1, :, PAD:top])[0]
    sy1[0] = sums(e1[:, :, top - 2 : top - 1], e1[:, :, top - 1 : top])[0]
    for x in range(2):
        sc1[x, 1] = sums(sx1[x, :, 0:1], sx1[x, :, 1:2])[1]
        sc1[x, 0] = sums(sx1[x, :, cy - 2 : cy - 1], sx1[x, :, cy - 1 : cy])[0]
    pl.semaphore_wait(barrier, len(greet))
    step = (1, -1)
    post_x = lambda x: post(sx1.at[x], hx1.at[x, :, pl.ds(PAD, cy), :], step[x], 0)
    post_y = lambda y: post(sy1.at[y], hy1.at[y], 0, step[y])
    post_c = lambda x, y: post(sc1.at[x, y], hc1.at[x, y], step[x], step[y])
    now1 = [post_c(1, 1), post_x(1), post_y(1)]
    later1 = [post_c(0, 1), post_c(1, 0), post_c(0, 0), post_x(0), post_y(0)]

    def place(ref, rows, side):
        if side == 0:
            ref[..., PAD - 2 : PAD - 1, :] = rows
            ref[..., PAD - 1 : PAD, :] = jnp.zeros_like(rows)
        else:
            ref[..., top : top + 1, :] = -ROOT3 * rows
            ref[..., top + 1 : top + 2, :] = rows

    def pair1(n):
        return sums(e1[2 * n], e1[2 * n + 1])

    for c in now1:
        c.wait_recv()
    place(e1, hy1[1], 1)
    place(hx1.at[1], hc1[1, 1], 1)

    def lift1(n, carry):
        smooth, part_n = pair1(n)
        before, _ = pair1(n - 1)
        detail = part_n - FAR * before
        xd1[n] = HIGH * detail
        xs1[n] = LOW * (before - detail)
        return carry

    lax.fori_loop(1, hx, lift1, 0)
    edge, _ = pair1(hx - 1)
    edge_d = hx1[1] - FAR * edge
    xd1[hx] = HIGH * edge_d
    xs1[hx] = LOW * (edge - edge_d)

    def coarse1(n, carry):
        for h in range(2):
            load = lambda start: xs1[n, h, pl.ds(start, hy, stride=2), :]
            s0, _ = sums(load(PAD), load(PAD + 1))
            _, tp = sums(load(PAD + 2), load(PAD + 3))
            s1s[n, h, PAD : PAD + hy] = LOW * (s0 - (tp - FAR * s0))
        return carry

    lax.fori_loop(1, hx + 1, coarse1, 0)

    def lines(ref, xs, ys):
        n = (xs.stop - xs.start) * (ys.stop - ys.start)
        return jnp.concatenate([ref[xs, h, ys].reshape(n, LANES) for h in range(2)], axis=1)

    chunk = hx // 2
    for i in range(2):
        rows = lines(s1s, slice(1 + i * chunk, 1 + (i + 1) * chunk), slice(PAD, PAD + hy))
        e2[4 + i * chunk : 4 + (i + 1) * chunk, PAD : PAD + hy] = times(
            rows, w1.at[:, :, 0:LANES]).reshape(chunk, hy, LANES)

    st2[...] = sums(e2[4, PAD : PAD + hy], e2[5, PAD : PAD + hy])[1]
    y_own, y_low, y_high = pl.ds(PAD, hy), pl.ds(0, PAD), pl.ds(PAD + hy, PAD)
    y_first, y_last = pl.ds(PAD, PAD), pl.ds(hy, PAD)
    own2, from2, to2 = pl.ds(4, hx), pl.ds(hx, 4), pl.ds(0, 4)
    now2 = [
        post(st2, ht2.at[y_own, :], -1, 0),
        post(e2.at[own2, y_first, :], e2.at[own2, y_high, :], 0, -1),
        post(st2.at[pl.ds(0, PAD), :], ht2.at[y_high, :], -1, -1),
    ]
    later2 = [
        post(e2.at[own2, y_last, :], e2.at[own2, y_low, :], 0, 1),
        post(e2.at[from2, y_own, :], e2.at[to2, y_own, :], 1, 0),
        post(e2.at[from2, y_last, :], e2.at[to2, y_low, :], 1, 1),
        post(e2.at[from2, y_first, :], e2.at[to2, y_high, :], 1, -1),
        post(st2.at[pl.ds(hy - PAD, PAD), :], ht2.at[y_low, :], -1, 1),
    ]

    for c in later1:
        c.wait_recv()
    place(e1, hy1[0], 0)
    place(hx1.at[1], hc1[1, 0], 0)
    place(hx1.at[0], hc1[0, 0], 0)
    place(hx1.at[0], hc1[0, 1], 1)
    first_s, first_t = pair1(0)
    first_d = first_t - FAR * hx1[0]
    xd1[0] = HIGH * first_d
    xs1[0] = LOW * (hx1[0] - first_d)
    low = slice(PAD - 2, PAD)

    def low1(n, carry):
        def pair(n):
            return sums(e1[2 * n, :, low], e1[2 * n + 1, :, low])
        _, part_n = pair(n)
        before, _ = pair(n - 1)
        detail = part_n - FAR * before
        xd1[n, :, low] = HIGH * detail
        xs1[n, :, low] = LOW * (before - detail)
        return carry

    lax.fori_loop(1, hx, low1, 0)
    edge, _ = sums(e1[cx - 2, :, low], e1[cx - 1, :, low])
    edge_d = hx1[1, :, low] - FAR * edge
    xd1[hx, :, low] = HIGH * edge_d
    xs1[hx, :, low] = LOW * (edge - edge_d)

    def cols1(n, carry):
        for h in range(2):
            for src, det, smo in ((xd1, d1d, d1s), (xs1, s1d, s1s)):
                load = lambda start: src[n, h, pl.ds(start, hy + 1, stride=2), :]
                s0, t0 = sums(load(PAD), load(PAD + 1))
                sm, _ = sums(load(PAD - 2), load(PAD - 1))
                d = t0 - FAR * sm
                det[n, h, 0 : hy + 1] = HIGH * d
                smo[n, h, PAD - 1 : PAD + hy] = LOW * (sm - d)
        return carry

    lax.fori_loop(0, hx + 1, cols1, 0)

    magnitude = jnp.zeros((PAD, LANES), jnp.float32)
    rows1 = hy + PAD
    for ref in (d1d, d1s, s1d, s1s):
        for lo, hi in ((0, chunk), (chunk, hx + 1)):
            rows = lines(ref, slice(lo, hi), slice(0, rows1))
            if ref is s1s:
                ref[lo:hi, 1] = times(rows, w1.at[:, :, LANES : 2 * LANES]).reshape(
                    hi - lo, rows1, LANES)
                continue
            got = times(rows, w1)
            for h in range(2):
                ref[lo:hi, h] = got[:, h * LANES : (h + 1) * LANES].reshape(hi - lo, rows1, LANES)
            if ref is d1d:
                mine = got[:, LANES:].reshape(hi - lo, rows1, LANES)[: chunk, :hy]
                magnitude = magnitude + jnp.sum(
                    jnp.abs(mine).reshape(chunk * hy // PAD, PAD, LANES), axis=0)
        if ref is d1d:
            part[0] = magnitude
            sums_x = [post(part.at[0], part.at[k], k, 0) for k in range(1, nx)]

    for c in now2:
        c.wait_recv()
    x2, yrows, pairs = qx + 2, qy + 2 * PAD, hy // 2 + PAD

    def lift2(rows):
        def step(n, carry):
            before, _ = sums(e2[2 * n, rows], e2[2 * n + 1, rows])
            _, part_n = sums(e2[2 * n + 2, rows], e2[2 * n + 3, rows])
            detail = part_n - FAR * before
            xd2[n, rows] = HIGH * detail
            xs2[n, rows] = LOW * (before - detail)
            return carry
        return step

    def last2(rows):
        before, _ = sums(e2[2 * x2 - 2, rows], e2[2 * x2 - 1, rows])
        detail = ht2[rows] - FAR * before
        xd2[x2 - 1, rows] = HIGH * detail
        xs2[x2 - 1, rows] = LOW * (before - detail)

    above, every = slice(PAD, hy + 2 * PAD), slice(0, hy + 2 * PAD)
    lax.fori_loop(2, x2 - 1, lift2(above), 0)
    last2(above)
    load2 = lambda start: xs2[2:x2, pl.ds(start, qy, stride=2), :]
    s0, _ = sums(load2(PAD), load2(PAD + 1))
    _, tp = sums(load2(PAD + 2), load2(PAD + 3))
    smooth2 = LOW * (s0 - (tp - FAR * s0))
    coarse2 = times(smooth2.reshape(qx * qy, LANES), w2)
    coarse2 = coarse2.reshape(qx // 2, 2, qy, LANES)
    lane = lax.broadcasted_iota(jnp.int32, (qx // 2, qy, LANES), 2)
    half = LANES // 2
    packed = jnp.where(lane < half, coarse2[:, 0], pltpu.roll(coarse2[:, 1], half, 2))
    ep3[2 : 2 + qx // 2, PAD : PAD + qy] = packed

    n_own = qx // 2
    own3 = pl.ds(2, n_own)
    z_own, z_low, z_high = pl.ds(PAD, qy), pl.ds(0, PAD), pl.ds(PAD + qy, PAD)
    z_first, z_last = pl.ds(PAD, PAD), pl.ds(qy, PAD)
    round3 = []
    for dx, xs, xd in ((1, pl.ds(n_own, 2), pl.ds(0, 2)),
                       (-1, pl.ds(2, 1), pl.ds(2 + n_own, 1)), (0, own3, own3)):
        for dy, ys, yd in ((0, z_own, z_own), (1, z_last, z_low), (-1, z_first, z_high)):
            if dx or dy:
                round3.append(post(ep3.at[xs, ys, :], ep3.at[xd, yd, :], dx, dy))

    for c in sums_x:
        c.wait_recv()
    acc = part[0]
    for k in range(1, nx):
        acc = acc + part[k]
    total[0] = acc
    sums_y = [post(total.at[0], total.at[k], 0, k) for k in range(1, ny)]

    for c in later2:
        c.wait_recv()
    lax.fori_loop(0, x2 - 1, lift2(every), 0)
    last2(every)

    def rows2(src, at):
        return forward_rows(src[at, pl.ds(0, pairs, stride=2), :],
                            src[at, pl.ds(1, pairs, stride=2), :])

    for src, det, smo in ((xd2, dd, ds), (xs2, sd, ss)):
        for band, dst in zip(rows2(src, slice(0, x2)), (det, smo)):
            dst[:, PAD // 2 : PAD // 2 + pairs] = times(
                band.reshape(x2 * pairs, LANES), w2).reshape(x2, pairs, LANES)

    for c in round3:
        c.wait_recv()
    low_s, low_t = [], []
    for n in range(n_own + 3):
        s, t = sums(ep3[n], pltpu.roll(ep3[n], half, 1))
        low_s.append(s)
        low_t.append(t)
    n3 = n_own + 2
    for n in range(n3):
        detail = low_t[n + 1] - FAR * low_s[n]
        t3d[n] = HIGH * detail
        t3s[n] = LOW * (low_s[n] - detail)
    h3 = qy // 2 + PAD
    bands = []
    for src in (t3d, t3s):
        bands += forward_rows(src[:, pl.ds(0, h3, stride=2), :], src[:, pl.ds(1, h3, stride=2), :])
    for i, band in enumerate(bands):
        bands[i] = times(band.reshape(n3 * h3, LANES), w3).reshape(n3, h3, LANES)

    for c in sums_y:
        c.wait_recv()
    acc = total[0]
    for k in range(1, ny):
        acc = acc + total[k]
    noise = jnp.sum(acc, axis=(0, 1), keepdims=True) * (math.sqrt(math.pi / 2.0) / count_all)

    lane3 = lax.broadcasted_iota(jnp.int32, (n3, h3, LANES), 2)
    noise3 = noise.reshape(1, 1, 1)
    b_dd, b_ds, b_sd = (shrink(b, noise3) for b in bands[:3])
    b_ss = jnp.where(lane3 < cz // 8, bands[3], shrink(bands[3], noise3))

    def inverse_x(det, smo):
        det, smo = det * (1.0 / HIGH), smo * (1.0 / LOW)
        one = smo + det
        even, odd = undo(det[:-1], one[1:], one[:-1])
        return weave(even, odd)

    y_d = inverse_x(b_dd, b_sd) * (1.0 / HIGH)
    y_s = inverse_x(b_ds, b_ss) * (1.0 / LOW)
    one = y_s + pltpu.roll(y_d, h3 - 1, 1)
    even, odd = undo(y_d, one, pltpu.roll(one, 1, 1))
    r2[:, pl.ds(0, h3, stride=2), :] = even
    r2[:, pl.ds(1, h3, stride=2), :] = odd
    back = times(r2[...].reshape(x2 * yrows, LANES), v3).reshape(x2, yrows, LANES)

    lane2 = lax.broadcasted_iota(jnp.int32, (x2, yrows, LANES), 2)
    ss[...] = jnp.where(lane2 < cz // 4, back, shrink(ss[...], noise3))

    def inv2(n, carry):
        def one_x(n):
            d_d = shrink(dd[n], noise) * (1.0 / HIGH)
            d_s = shrink(ds[n], noise) * (1.0 / HIGH)
            s_d = shrink(sd[n], noise) * (1.0 / LOW)
            s_s = ss[n] * (1.0 / LOW)
            return d_d, d_s, s_d + d_d, s_s + d_s

        d_d, d_s, b_d, b_s = one_x(n)
        _, _, f_d, f_s = one_x(n + 1)
        pair_d = undo(d_d, f_d, b_d)
        pair_s = undo(d_s, f_s, b_s)
        for i in range(2):
            y_d, y_s = pair_d[i] * (1.0 / HIGH), pair_s[i] * (1.0 / LOW)
            one = y_s + pltpu.roll(y_d, yrows - 1, 0)
            even, odd = undo(y_d, one, pltpu.roll(one, 1, 0))
            r1[2 * n + i, pl.ds(0, yrows, stride=2), :] = even
            r1[2 * n + i, pl.ds(1, yrows, stride=2), :] = odd
        return carry

    lax.fori_loop(0, qx + 1, inv2, 0)
    x1, y1 = hx + 2, hy + PAD
    back = times(r1[:, PAD : PAD + y1].reshape(x1 * y1, LANES), v2).reshape(x1, y1, LANES)
    s1s[:, 0] = back[1:]

    def inv1(n, carry):
        for h in range(2):
            for det, smo, dst in ((d1d, s1d, p1d), (d1s, s1s, p1s)):
                plain = smo is s1s and h == 0

                def one_x(n):
                    d = shrink(det[n, h], noise) * (1.0 / HIGH)
                    s = smo[n, h] if plain else shrink(smo[n, h], noise)
                    return d, s * (1.0 / LOW) + d

                d, before = one_x(n)
                _, one = one_x(n + 1)
                even, odd = undo(d, one, before)
                dst[2 * n, h] = even
                dst[2 * n + 1, h] = odd
        return carry

    lax.fori_loop(0, hx, inv1, 0)

    def inv1_y(n, carry):
        for h in range(2):
            y_d = p1d[n, h, 0:hy] * (1.0 / HIGH)
            y_n = p1d[n, h, 1 : hy + 1] * (1.0 / HIGH)
            s = p1s[n, h, PAD : PAD + hy] * (1.0 / LOW)
            s_b = p1s[n, h, PAD - 1 : PAD - 1 + hy] * (1.0 / LOW)
            even, odd = undo(y_d, s + y_n, s_b + y_d)
            o1[n, h, pl.ds(0, hy, stride=2), :] = even
            o1[n, h, pl.ds(1, hy, stride=2), :] = odd
        return carry

    lax.fori_loop(0, cx, inv1_y, 0)
    layers = 8
    outs = []
    for i in range(cx // layers):
        xs = slice(i * layers, (i + 1) * layers)
        rows = jnp.concatenate(
            [o1[xs, h].reshape(layers * cy, LANES) for h in range(2)], axis=1)
        ob[xs] = times(rows, v1).reshape(layers, cy, cz)
        c = pltpu.make_async_copy(ob.at[xs], out.at[xs], osem.at[i])
        c.start()
        outs.append(c)
    for c in outs:
        c.wait()
    for c in started:
        c.wait_send()


def on_device(nx, ny, volume):
    cx, cy, cz = volume.shape
    hx, hy, qx, qy = cx // 2, cy // 2, cx // 4, cy // 4
    n3, h3 = qx // 2 + 2, qy // 2 + PAD
    f32 = jnp.float32
    count = cx * nx * cy * ny * cz // 8
    weights = [
        halves(forward_matrix(cz), cz), halves(forward_matrix(cz // 2), LANES),
        halves(forward_matrix(cz // 4), LANES), halves(inverse_matrix(cz), cz),
        halves(inverse_matrix(cz // 2), LANES), halves(inverse_matrix(cz // 4), LANES),
    ]
    messages = 24 + nx - 1 + ny - 1
    vmem = lambda *s: pltpu.VMEM(s, f32)
    ey, ey2, ey3 = cy + 2 * PAD, hy + 2 * PAD, qy + 2 * PAD
    scratch = [
        vmem(cx, 2, ey, LANES), vmem(2, 2, ey, LANES), vmem(2, 2, cy, LANES),
        vmem(2, cx, 2, 1, LANES), vmem(2, cx, 2, 1, LANES),
        vmem(2, 2, 2, 1, LANES), vmem(2, 2, 2, 1, LANES),
        vmem(hx + 1, 2, ey, LANES), vmem(hx + 1, 2, ey, LANES),
        *[vmem(hx + 1, 2, hy + PAD, LANES) for _ in range(4)],
        vmem(hx + 4, ey2, LANES), vmem(ey2, LANES), vmem(hy, LANES),
        vmem(qx + 2, ey2, LANES), vmem(qx + 2, ey2, LANES),
        *[vmem(qx + 2, ey3, LANES) for _ in range(4)],
        vmem(qx // 2 + 3, ey3, LANES),
        vmem(n3, ey3, LANES), vmem(n3, ey3, LANES),
        vmem(qx + 2, ey3, LANES),
        vmem(hx + 2, 2 * ey3, LANES),
        vmem(cx, 2, hy + PAD, LANES), vmem(cx, 2, hy + PAD, LANES),
        vmem(cx, 2, cy, LANES), vmem(cx, cy, cz),
        vmem(nx, PAD, LANES), vmem(ny, PAD, LANES),
        pltpu.SemaphoreType.DMA((messages,)), pltpu.SemaphoreType.DMA((messages,)),
        pltpu.SemaphoreType.DMA((2,)), pltpu.SemaphoreType.DMA((cx // 8,)),
    ]
    return pl.pallas_call(
        functools.partial(kernel, (cx, cy, cz), count, nx, ny),
        out_shape=jax.ShapeDtypeStruct(volume.shape, f32),
        in_specs=[pl.BlockSpec(memory_space=pl.ANY)]
        + [pl.BlockSpec(memory_space=pltpu.VMEM)] * 6,
        out_specs=pl.BlockSpec(memory_space=pl.ANY),
        scratch_shapes=scratch,
        compiler_params=pltpu.CompilerParams(
            collective_id=0, has_side_effects=True, vmem_limit_bytes=56 * 1024 * 1024),
    )(volume, *[jnp.asarray(w) for w in weights])


def solution(mesh):
    spec = P("gx", "gy", None)
    body = functools.partial(on_device, mesh.shape["gx"], mesh.shape["gy"])
    return jax.shard_map(body, mesh=mesh, in_specs=(spec,), out_specs=spec, check_vma=False)
```

time: 41.7 us -> 31.2 us (0.75)
  Pallas kernels: 38.4 us -> 27.8 us
    pallas_call x1, Pallas kernels: 38.4 us -> 27.8 us  [on_device(): pl.pallas_call(functools.partial(kernel, (cx, cy, cz), count, nx, ny), ou...]
where the time goes in v1:
time: 31.2 us; the launch traced here: 31 us
  Pallas kernels  27.8 us (89%)
  local copies, waits for them, and re-layouts  3.13 us (10%)
    pallas_call x1, Pallas kernels, on_device(): pl.pallas_call(functools.partial(kernel, (cx, cy, cz), count, nx, ny), ou...  27.8 us
    unnamed x1, local copies, waits for them, and re-layouts  3.13 us

profile of v1, /device:TPU:0, one launch (start us, length us, event | category | flops | bytes accessed | tf_op | source)
XLA Modules:
  0.0 31.0 jit_solution(6811418496737683010)
XLA Ops:
  0.0 27.8 %shard_map.73 = f32[32,64,256]{2,1,0:T(8,128)} custom-call(f32[32,64,256]{2,1,0:T(8,128)} %vol.1, bf16[2,256,256]{2,1,0:T(8,128)(2,1)} %constant.12.clone.w1, bf16[2,128,128]{2,1,0:T(8,128)(2,1)} %constant.13.clone.w2, bf16[2,128,128]{2,1,0:T(8,128)(2,1)} %constant.14.clone.w3, bf16[2,256,256]{2,1,0:T(8,128)(2,1)} %constant.15.clone.v1, ...), custom_call_target="tpu_custom_call" | custom-call | tf_op jit(solution)/shard_map/pallas_call | solution.py:487
  27.8 3.1 %copy.9 = f32[32,64,256]{2,1,0:T(8,128)} copy(f32[32,64,256]{2,1,0:T(8,128)} %shard_map.73) | data formatting | bytes 4194304

commit v2 on v1

--- a/solution.py
+++ b/solution.py
@@ -77,10 +77,11 @@
     return HIGH * detail, LOW * (smooth - pltpu.roll(detail, even.shape[axis] - 1, axis))
 
 
-def kernel(shape, count_all, nx, ny, vol, w1, w2, w3, v1, v2, v3, out,
+def kernel(shape, count_all, nx, ny, vol, g1, g2, g3, g4, g5, g6, o1, v1,
+           w1, w2, w3, v2, v3,
            e1, hx1, sx1, hy1, sy1, hc1, sc1, xd1, xs1, s1s, s1d, d1s, d1d,
            e2, ht2, st2, xd2, xs2, ss, sd, ds, dd, ep3, t3d, t3s, r2, r1,
-           p1s, p1d, o1, ob, part, total, send, recv, lsem, osem):
+           p1s, p1d, part, total, send, recv, lsem, wsem):
     cx, cy, cz = shape
     hx, hy, qx, qy = cx // 2, cy // 2, cx // 4, cy // 4
     ix, iy = lax.axis_index("gx"), lax.axis_index("gy")
@@ -94,7 +95,12 @@
             e1.at[:, h, pl.ds(PAD, cy), :], lsem.at[h])
         for h in range(2)
     ]
-    for c in loads:
+    weights = [
+        pltpu.make_async_copy(src, dst, wsem.at[i])
+        for i, (src, dst) in enumerate(
+            zip((g1, g2, g3, g4, g5, g6), (w1, w2, w3, v1, v2, v3)))
+    ]
+    for c in loads + weights:
         c.start()
 
     greet = [(dx, dy) for dx in (-1, 0, 1) for dy in (-1, 0, 1) if dx or dy]
@@ -175,6 +181,8 @@
         return carry
 
     lax.fori_loop(1, hx + 1, coarse1, 0)
+    for c in weights:
+        c.wait()
 
     def lines(ref, xs, ys):
         n = (xs.stop - xs.start) * (ys.stop - ys.start)
@@ -231,23 +239,25 @@
     xd1[hx, :, low] = HIGH * edge_d
     xs1[hx, :, low] = LOW * (edge - edge_d)
 
-    def cols1(n, carry):
-        for h in range(2):
-            for src, det, smo in ((xd1, d1d, d1s), (xs1, s1d, s1s)):
+    def cols1(src, det, smo):
+        def step(n, carry):
+            for h in range(2):
                 load = lambda start: src[n, h, pl.ds(start, hy + 1, stride=2), :]
                 s0, t0 = sums(load(PAD), load(PAD + 1))
                 sm, _ = sums(load(PAD - 2), load(PAD - 1))
                 d = t0 - FAR * sm
                 det[n, h, 0 : hy + 1] = HIGH * d
                 smo[n, h, PAD - 1 : PAD + hy] = LOW * (sm - d)
-        return carry
-
-    lax.fori_loop(0, hx + 1, cols1, 0)
-
-    magnitude = jnp.zeros((PAD, LANES), jnp.float32)
+            return carry
+
+        lax.fori_loop(0, hx + 1, step, 0)
+
     rows1 = hy + PAD
-    for ref in (d1d, d1s, s1d, s1s):
-        for lo, hi in ((0, chunk), (chunk, hx + 1)):
+    parts1 = ((0, chunk), (chunk, hx + 1))
+
+    def depth1(ref):
+        magnitude = jnp.zeros((PAD, LANES), jnp.float32)
+        for lo, hi in parts1:
             rows = lines(ref, slice(lo, hi), slice(0, rows1))
             if ref is s1s:
                 ref[lo:hi, 1] = times(rows, w1.at[:, :, LANES : 2 * LANES]).reshape(
@@ -257,12 +267,14 @@
             for h in range(2):
                 ref[lo:hi, h] = got[:, h * LANES : (h + 1) * LANES].reshape(hi - lo, rows1, LANES)
             if ref is d1d:
-                mine = got[:, LANES:].reshape(hi - lo, rows1, LANES)[: chunk, :hy]
+                mine = got[:, LANES:].reshape(hi - lo, rows1, LANES)[:chunk, :hy]
                 magnitude = magnitude + jnp.sum(
                     jnp.abs(mine).reshape(chunk * hy // PAD, PAD, LANES), axis=0)
-        if ref is d1d:
-            part[0] = magnitude
-            sums_x = [post(part.at[0], part.at[k], k, 0) for k in range(1, nx)]
+        return magnitude
+
+    cols1(xd1, d1d, d1s)
+    part[0] = depth1(d1d)
+    sums_x = [post(part.at[0], part.at[k], k, 0) for k in range(1, nx)]
 
     for c in now2:
         c.wait_recv()
@@ -309,6 +321,9 @@
             if dx or dy:
                 round3.append(post(ep3.at[xs, ys, :], ep3.at[xd, yd, :], dx, dy))
 
+    cols1(xs1, s1d, s1s)
+    depth1(d1s)
+
     for c in sums_x:
         c.wait_recv()
     acc = part[0]
@@ -316,6 +331,9 @@
         acc = acc + part[k]
     total[0] = acc
     sums_y = [post(total.at[0], total.at[k], 0, k) for k in range(1, ny)]
+
+    depth1(s1d)
+    depth1(s1s)
 
     for c in later2:
         c.wait_recv()
@@ -435,20 +453,24 @@
         return carry
 
     lax.fori_loop(0, cx, inv1_y, 0)
+    for c in started:
+        c.wait_send()
+
+
+def finish(rows_in, v1, out, ob, osem):
+    cx, cy, cz = out.shape
     layers = 8
     outs = []
     for i in range(cx // layers):
         xs = slice(i * layers, (i + 1) * layers)
         rows = jnp.concatenate(
-            [o1[xs, h].reshape(layers * cy, LANES) for h in range(2)], axis=1)
+            [rows_in[xs, h].reshape(layers * cy, LANES) for h in range(2)], axis=1)
         ob[xs] = times(rows, v1).reshape(layers, cy, cz)
         c = pltpu.make_async_copy(ob.at[xs], out.at[xs], osem.at[i])
         c.start()
         outs.append(c)
     for c in outs:
         c.wait()
-    for c in started:
-        c.wait_send()
 
 
 def on_device(nx, ny, volume):
@@ -465,7 +487,9 @@
     messages = 24 + nx - 1 + ny - 1
     vmem = lambda *s: pltpu.VMEM(s, f32)
     ey, ey2, ey3 = cy + 2 * PAD, hy + 2 * PAD, qy + 2 * PAD
+    wide = lambda n: pltpu.VMEM((2, n, n), jnp.bfloat16)
     scratch = [
+        wide(cz), wide(LANES), wide(LANES), wide(LANES), wide(LANES),
         vmem(cx, 2, ey, LANES), vmem(2, 2, ey, LANES), vmem(2, 2, cy, LANES),
         vmem(2, cx, 2, 1, LANES), vmem(2, cx, 2, 1, LANES),
         vmem(2, 2, 2, 1, LANES), vmem(2, 2, 2, 1, LANES),
@@ -479,21 +503,28 @@
         vmem(qx + 2, ey3, LANES),
         vmem(hx + 2, 2 * ey3, LANES),
         vmem(cx, 2, hy + PAD, LANES), vmem(cx, 2, hy + PAD, LANES),
-        vmem(cx, 2, cy, LANES), vmem(cx, cy, cz),
         vmem(nx, PAD, LANES), vmem(ny, PAD, LANES),
         pltpu.SemaphoreType.DMA((messages,)), pltpu.SemaphoreType.DMA((messages,)),
-        pltpu.SemaphoreType.DMA((2,)), pltpu.SemaphoreType.DMA((cx // 8,)),
+        pltpu.SemaphoreType.DMA((2,)), pltpu.SemaphoreType.DMA((6,)),
     ]
-    return pl.pallas_call(
+    near = pl.BlockSpec(memory_space=pltpu.VMEM)
+    rows, v1 = pl.pallas_call(
         functools.partial(kernel, (cx, cy, cz), count, nx, ny),
-        out_shape=jax.ShapeDtypeStruct(volume.shape, f32),
-        in_specs=[pl.BlockSpec(memory_space=pl.ANY)]
-        + [pl.BlockSpec(memory_space=pltpu.VMEM)] * 6,
-        out_specs=pl.BlockSpec(memory_space=pl.ANY),
+        out_shape=(pltpu.VMEM((cx, 2, cy, LANES), f32), wide(cz)),
+        in_specs=[pl.BlockSpec(memory_space=pltpu.HBM)] * 7,
+        out_specs=(near, near),
         scratch_shapes=scratch,
         compiler_params=pltpu.CompilerParams(
             collective_id=0, has_side_effects=True, vmem_limit_bytes=56 * 1024 * 1024),
     )(volume, *[jnp.asarray(w) for w in weights])
+    return pl.pallas_call(
+        finish,
+        out_shape=jax.ShapeDtypeStruct(volume.shape, f32),
+        in_specs=[near, near],
+        out_specs=pl.BlockSpec(memory_space=pltpu.HBM),
+        scratch_shapes=[vmem(cx, cy, cz), pltpu.SemaphoreType.DMA((cx // 8,))],
+        compiler_params=pltpu.CompilerParams(vmem_limit_bytes=16 * 1024 * 1024),
+    )(rows, v1)
 
 
 def solution(mesh):

time: 31.2 us -> 26.7 us (0.86)
  local copies, waits for them, and re-layouts: 3.13 us -> 0 us
  Pallas kernels: 27.8 us -> 26.6 us
    pallas_call x1, Pallas kernels: 27.8 us -> 24.5 us  [on_device(): pl.pallas_call(functools.partial(kernel, (cx, cy, cz), count, nx, ny), ou...]
    unnamed x1 -> x0, local copies, waits for them, and re-layouts: 3.13 us -> none
    pallas_call x0 -> x1, Pallas kernels: none -> 2.03 us  [on_device(): pl.pallas_call(finish, out_shape=jax.ShapeDtypeStruct(volume.shape, f32),...]
where the time goes in v2:
time: 26.7 us; the launch traced here: 26.6 us
  Pallas kernels  26.6 us (100%)
    pallas_call x1, Pallas kernels, on_device(): pl.pallas_call(functools.partial(kernel, (cx, cy, cz), count, nx, ny), ou...  24.5 us
    pallas_call x1, Pallas kernels, on_device(): pl.pallas_call(finish, out_shape=jax.ShapeDtypeStruct(volume.shape, f32),...  2.03 us

profile of v2, /device:TPU:0, one launch (start us, length us, event | category | flops | bytes accessed | tf_op | source)
XLA Modules:
  0.0 26.6 jit_solution(9117513586822686794)
XLA Ops:
  0.0 24.5 %shard_map.73 = (f32[32,2,64,128]{3,2,1,0:T(8,128)S(1)}, bf16[2,256,256]{2,1,0:T(8,128)(2,1)S(1)}) custom-call(f32[32,64,256]{2,1,0:T(8,128)} %vol.1, bf16[2,256,256]{2,1,0:T(8,128)(2,1)} %constant.12.clone.g1, bf16[2,128,128]{2,1,0:T(8,128)(2,1)} %constant.13.clone.g2, bf16[2,128,128]{2,1,0:T(8,128)(2,1)} %constant.14.clone.g3, ...), custom_call_target="tpu_custom_call" | custom-call | tf_op jit(solution)/shard_map/pallas_call | solution.py:511
  24.5 2.0 %shard_map.74 = f32[32,64,256]{2,1,0:T(8,128)} custom-call(f32[32,2,64,128]{3,2,1,0:T(8,128)S(1)} %get-tuple-element.7.rows_in, bf16[2,256,256]{2,1,0:T(8,128)(2,1)S(1)} %get-tuple-element.8.v1), custom_call_target="tpu_custom_call" | custom-call | tf_op jit(solution)/shard_map/pallas_call | solution.py:520

commit v3 on v2

--- a/solution.py
+++ b/solution.py
@@ -150,39 +150,50 @@
             ref[..., top : top + 1, :] = -ROOT3 * rows
             ref[..., top + 1 : top + 2, :] = rows
 
-    def pair1(n):
-        return sums(e1[2 * n], e1[2 * n + 1])
-
+    def pair1(n, rows=slice(None)):
+        return sums(e1[2 * n, :, rows], e1[2 * n + 1, :, rows])
+
+    def lift1(rows):
+        def step(n, carry):
+            _, part_n = pair1(n, rows)
+            before, _ = pair1(n - 1, rows)
+            detail = part_n - FAR * before
+            xd1[n, :, rows] = HIGH * detail
+            xs1[n, :, rows] = LOW * (before - detail)
+            return carry
+
+        lax.fori_loop(1, hx, step, 0)
+
+    def coarse1(n, first, count):
+        for h in range(2):
+            load = lambda start: xs1[n, h, pl.ds(start + 2 * first, count, stride=2), :]
+            s0, _ = sums(load(PAD), load(PAD + 1))
+            _, tp = sums(load(PAD + 2), load(PAD + 3))
+            s1s[n, h, PAD + first : PAD + first + count] = LOW * (s0 - (tp - FAR * s0))
+
+    def coarse1_inner(n, carry):
+        coarse1(n, 0, hy)
+        return carry
+
+    def coarse1_top(n, carry):
+        coarse1(n, hy - 1, 1)
+        return carry
+
+    lift1(slice(PAD, top))
+    lax.fori_loop(1, hx, coarse1_inner, 0)
+    for c in weights:
+        c.wait()
     for c in now1:
         c.wait_recv()
     place(e1, hy1[1], 1)
     place(hx1.at[1], hc1[1, 1], 1)
-
-    def lift1(n, carry):
-        smooth, part_n = pair1(n)
-        before, _ = pair1(n - 1)
-        detail = part_n - FAR * before
-        xd1[n] = HIGH * detail
-        xs1[n] = LOW * (before - detail)
-        return carry
-
-    lax.fori_loop(1, hx, lift1, 0)
+    lift1(slice(top, top + 2))
     edge, _ = pair1(hx - 1)
     edge_d = hx1[1] - FAR * edge
     xd1[hx] = HIGH * edge_d
     xs1[hx] = LOW * (edge - edge_d)
-
-    def coarse1(n, carry):
-        for h in range(2):
-            load = lambda start: xs1[n, h, pl.ds(start, hy, stride=2), :]
-            s0, _ = sums(load(PAD), load(PAD + 1))
-            _, tp = sums(load(PAD + 2), load(PAD + 3))
-            s1s[n, h, PAD : PAD + hy] = LOW * (s0 - (tp - FAR * s0))
-        return carry
-
-    lax.fori_loop(1, hx + 1, coarse1, 0)
-    for c in weights:
-        c.wait()
+    lax.fori_loop(1, hx, coarse1_top, 0)
+    coarse1(hx, 0, hy)
 
     def lines(ref, xs, ys):
         n = (xs.stop - xs.start) * (ys.stop - ys.start)
@@ -223,17 +234,7 @@
     xs1[0] = LOW * (hx1[0] - first_d)
     low = slice(PAD - 2, PAD)
 
-    def low1(n, carry):
-        def pair(n):
-            return sums(e1[2 * n, :, low], e1[2 * n + 1, :, low])
-        _, part_n = pair(n)
-        before, _ = pair(n - 1)
-        detail = part_n - FAR * before
-        xd1[n, :, low] = HIGH * detail
-        xs1[n, :, low] = LOW * (before - detail)
-        return carry
-
-    lax.fori_loop(1, hx, low1, 0)
+    lift1(low)
     edge, _ = sums(e1[cx - 2, :, low], e1[cx - 1, :, low])
     edge_d = hx1[1, :, low] - FAR * edge
     xd1[hx, :, low] = HIGH * edge_d

time: 26.7 us -> 26.2 us (0.981)
  Pallas kernels: 26.6 us -> 26 us
    pallas_call x1, Pallas kernels: 24.5 us -> 24 us  [on_device(): pl.pallas_call(functools.partial(kernel, (cx, cy, cz), count, nx, ny), ou...]
where the time goes in v3:
time: 26.2 us; the launch traced here: 26 us
  Pallas kernels  26 us (99%)
    pallas_call x1, Pallas kernels, on_device(): pl.pallas_call(functools.partial(kernel, (cx, cy, cz), count, nx, ny), ou...  24 us
    pallas_call x1, Pallas kernels, on_device(): pl.pallas_call(finish, out_shape=jax.ShapeDtypeStruct(volume.shape, f32),...  2.03 us

profile of v3, /device:TPU:0, one launch (start us, length us, event | category | flops | bytes accessed | tf_op | source)
XLA Modules:
  0.0 26.0 jit_solution(14508042495764206399)
XLA Ops:
  0.0 24.0 %shard_map.73 = (f32[32,2,64,128]{3,2,1,0:T(8,128)S(1)}, bf16[2,256,256]{2,1,0:T(8,128)(2,1)S(1)}) custom-call(f32[32,64,256]{2,1,0:T(8,128)} %vol.1, bf16[2,256,256]{2,1,0:T(8,128)(2,1)} %constant.12.clone.g1, bf16[2,128,128]{2,1,0:T(8,128)(2,1)} %constant.13.clone.g2, bf16[2,128,128]{2,1,0:T(8,128)(2,1)} %constant.14.clone.g3, ...), custom_call_target="tpu_custom_call" | custom-call | tf_op jit(solution)/shard_map/pallas_call | solution.py:512
  24.0 2.0 %shard_map.74 = f32[32,64,256]{2,1,0:T(8,128)} custom-call(f32[32,2,64,128]{3,2,1,0:T(8,128)S(1)} %get-tuple-element.7.rows_in, bf16[2,256,256]{2,1,0:T(8,128)(2,1)S(1)} %get-tuple-element.8.v1), custom_call_target="tpu_custom_call" | custom-call | tf_op jit(solution)/shard_map/pallas_call | solution.py:521
